TPU v7x, 128 devices: a whole 4x4x4 slice. The times are simulated.
128 devices in a mesh: lat: 32 (over x, y, core), lon: 4 (over z).
Axes of the slice: x: 4, y: 4, z: 4, core: 2. Of those that a mesh axis runs over, the one named last changes fastest.
Arguments:
- coeffs_old: float32 [640, 2, 3, 50, 640], P(('lat', 'lon')), may hold values from -0.16 to 0.16
- noise: bfloat16 [640, 2, 3, 50, 640], P(('lat', 'lon')), may hold values from -6 to 6
- legendre: float32 [640, 640, 640], P(('lat', 'lon')), may hold values from -0.25 to 0.25
- decay: float32 [3], replicated, may hold values from 0.3 to 0.97
- amplitude: float32 [3, 640], replicated, may hold values from 0.005 to 0.05
- wavenumber_of_slot: int32 [640], replicated, may hold values from 0 to 639, as said below
- lat_order: int32 [640], replicated, may hold values from 0 to 639, each once
Outputs:
- coeffs_new: float32 [640, 2, 3, 50, 640], P(('lat', 'lon'))
- pattern: float32 [640, 50, 1280], P(('lat', 'lon'))
Inputs may be any that keep to these rules, and one draw needn't show every extreme that they name: `wavenumber_of_slot`: every wavenumber fills exactly one slot; the sums of the wavenumbers of one device's 5 slots differ between devices by less than 128. `lat_order`: every latitude stands in exactly one row.
All inputs are finite; a program needn't handle non-finite values.
Results may differ from a plain program's by a relative error of at most 0.0003.
Values sent between devices are 32-bit elements; how exact they have to be, the bound alone decides.
No kernel may reach another device: no remote copies, remote signals or barrier semaphores. Data moves between devices by JAX's collectives and lax.ppermute only.
A program may use at most 128 MiB of HBM per device.

v0:
```python
import jax
import jax.numpy as jnp
from jax import lax
from jax.sharding import PartitionSpec as P

LON = 1280


TWO_PI = 6.283185307179586


def evolve(coeffs_old, noise, decay, amplitude, waves):
    width = coeffs_old.shape[4]
    offsets = lax.broadcasted_iota(jnp.int32, (waves.shape[0], width), 1)
    live = waves[:, None] + offsets < width
    padded = jnp.concatenate([amplitude, jnp.zeros_like(amplitude)], axis=1)
    spread = jax.vmap(lambda wave: lax.dynamic_slice_in_dim(padded, wave, width, 1))(waves)
    factor = jnp.sqrt(1.0 - decay * decay)
    fresh = decay[None, None, :, None, None] * coeffs_old + (spread * factor[None, :, None])[
        :, None, :, None, :
    ] * noise.astype(jnp.float32)
    return jnp.where(live[:, None, None, None, :], fresh, jnp.zeros_like(fresh))


def synthesis_table(waves, length):
    column = lax.broadcasted_iota(jnp.int32, (waves.shape[0], length), 1)
    phase = waves[:, None] * column % length
    angle = phase.astype(jnp.float32) * (TWO_PI / length)
    weight = jnp.where(waves == 0, 1.0, 2.0).astype(jnp.float32)[:, None]
    return jnp.stack([weight * jnp.cos(angle), -weight * jnp.sin(angle)], axis=1)


def synthesize(values, table):
    return jnp.einsum("sreq,srl->qel", values, table, precision=lax.Precision.HIGHEST)


def local(coeffs_old, noise, legendre, decay, amplitude, wavenumber_of_slot, lat_order):
    lat_count = lax.axis_size("lat")
    lon_count = lax.axis_size("lon")
    lat_index = lax.axis_index("lat")
    lon_index = lax.axis_index("lon")
    slots = coeffs_old.shape[0]
    mine = lax.dynamic_slice_in_dim(
        wavenumber_of_slot, (lat_index * lon_count + lon_index) * slots, slots
    )
    coeffs_new = evolve(coeffs_old, noise, decay, amplitude, mine)
    field = jnp.einsum("srkej,slj->srel", coeffs_new, legendre, precision=lax.Precision.HIGHEST)
    field = jnp.take(field, lat_order, axis=3)
    ordered = wavenumber_of_slot.reshape(lat_count, lon_count, slots).transpose(1, 0, 2).reshape(-1)
    full_table = synthesis_table(ordered, LON)
    pattern = synthesize(
        lax.all_to_all(
            lax.all_to_all(field, "lat", split_axis=3, concat_axis=0, tiled=True),
            "lon",
            split_axis=3,
            concat_axis=0,
            tiled=True,
        ),
        full_table,
    )
    return (coeffs_new, pattern)


def solution(mesh):
    in_specs = (
        P(("lat", "lon"), None, None, None, None),
        P(("lat", "lon"), None, None, None, None),
        P(("lat", "lon"), None, None),
        P(),
        P(),
        P(),
        P(),
    )
    out_specs = (P(("lat", "lon"), None, None, None, None), P(("lat", "lon"), None, None))
    return jax.shard_map(local, mesh=mesh, in_specs=in_specs, out_specs=out_specs, check_vma=False)
```

profile of v0, /device:TPU:1, one launch (start us, length us, event | category | flops | bytes accessed | tf_op | source)
XLA Modules:
  0.0 150.4 jit_solution(14142262357541582796)
XLA Ops:
  0.6 0.7 compare_and_fusion
  1.3 0.7 compare_select_fusion
  2.0 0.7 subtract_sqrt_fusion
  2.7 0.8 fusion.12
  3.5 0.1 add_compare_fusion
  3.5 0.7 concatenate.6
  4.2 6.6 %while.1 = (s32[]{:T(128)}, f32[3,1280]{1,0:T(4,128)S(1)}, s32[5,2]{0,1:T(2,128)S(1)}, f32[5,3,640]{2,1,0:T(4,128)S(1)}, s32[]{:T(128)}) while((s32[]{:T(128)}, f32[3,1280]{1,0:T(4,128)S(1)}, s32[5,2]{0,1:T(2,128)S(1)}, f32[5,3,640]{2,1,0:T(4,128)S(1)}, s32[]{:T(128)}) %tuple.24), condition=%wide.while_cond, body=%wide.while_body.sunk | while | flops 2 | bytes 20585 | solution.py:17
  4.2 0.1 constant_dynamic-slice_fusion.2
  4.3 0.5 slice.14
  4.8 0.7 bitcast_dynamic-update-slice_fusion.2
  5.6 0.1 constant_dynamic-slice_fusion.2
  5.6 0.5 slice.14
  6.2 0.7 bitcast_dynamic-update-slice_fusion.2
  6.9 0.1 constant_dynamic-slice_fusion.2
  7.0 0.5 slice.14
  7.5 0.7 bitcast_dynamic-update-slice_fusion.2
  8.2 0.1 constant_dynamic-slice_fusion.2
  8.3 0.5 slice.14
  8.8 0.7 bitcast_dynamic-update-slice_fusion.2
  9.5 0.1 constant_dynamic-slice_fusion.2
  9.6 0.5 slice.14
  10.1 0.7 bitcast_dynamic-update-slice_fusion.2
  10.8 0.1 broadcast_multiply_fusion
  10.9 0.0 copy-start
  10.9 9.0 %fusion.15 = (f32[5,2,50,640]{3,1,2,0:T(2,128)S(1)}, f32[5,2,3,50,640]{4,1,3,2,0:T(2,128)}) fusion(bf16[5,2,3,50,640]{4,1,3,2,0:T(2,128)(2,1)} %param.8, f32[5,3,640]{2,1,0:T(4,128)S(1)} %broadcast_multiply_fusion, f32[5,2,3,50,640]{4,1,3,2,0:T(2,128)} %param.7, f32[3]{0:T(128)} %param.10, pred[5,640]{1,0:T(8,128)(4,1)S(1)} %add_compare_fusion), kind=kLoop, calls=%fused_computation.33 | loop fusion | flops 5440000 | bytes 10921612 | tf_op jit(solution)/shard_map/srkej,slj->srel/reduce_sum | solution.py:47
  19.9 0.0 copy-done
  19.9 9.3 %fusion = f32[5,2,50,640]{3,2,1,0:T(8,128)} fusion(f32[5,640,640]{2,1,0:T(8,128)S(1)} %copy-done, f32[5,2,50,640]{3,1,2,0:T(2,128)S(1)} %get-tuple-element.18), kind=kOutput, calls=%fused_computation.3 | convolution fusion | flops 2457600000 | bytes 10752000 | tf_op jit(solution)/shard_map/srkej,slj->srel/dot_general | solution.py:47
  29.2 3.8 %copy.18 = f32[5,2,50,640]{2,1,3,0:T(2,128)S(1)} copy(f32[5,2,50,640]{3,2,1,0:T(8,128)} %fusion) | data formatting | bytes 2560000 | tf_op jit(solution)/shard_map/srkej,slj->srel/dot_general | solution.py:47
  33.0 7.3 %gather_fusion = f32[640,5,2,50]{3,2,1,0:T(2,128)} fusion(f32[5,2,50,640]{2,1,3,0:T(2,128)S(1)} %copy.18, s32[1024]{0:T(1024)S(1)} %pad_clamp_fusion), kind=kCustom, calls=%fused_computation | custom fusion | bytes 2562560 | tf_op jit(solution)/shard_map/jit(_take)/gather | solution.py:48
  40.3 4.2 %fusion.16 = f32[640,5,2,50]{3,2,1,0:T(2,128)S(1)} fusion(f32[640,5,2,50]{3,2,1,0:T(2,128)} %gather_fusion, pred[640]{0:T(1024)(128)(4,1)S(1)} %compare_and_fusion), kind=kLoop, calls=%fused_computation.34 | loop fusion | flops 320000 | bytes 2560640
  44.6 6.6 %reshape.218 = f32[32,1,10000]{2,1,0:T(1,128)} reshape(f32[640,5,2,50]{3,2,1,0:T(2,128)S(1)} %fusion.16) | data formatting | bytes 2560000
  51.1 28.6 %all_to_all.36 = f32[32,1,10000]{2,1,0:T(1,128)S(1)} all-to-all(f32[32,1,10000]{2,1,0:T(1,128)} %reshape.218), channel_id=1, replica_groups=mesh['lat'=32,'lon'=4] {'lat'}, dimensions={0} | all-to-all | bytes 2560000 | tf_op jit(solution)/shard_map/all_to_all | solution.py:53
  79.7 0.5 broadcast.203
  80.3 5.0 %reduce = f32[32,10000]{1,0:T(8,128)} reduce(f32[32,1,10000]{2,1,0:T(1,128)S(1)} %all_to_all.36, f32[]{:T(128)} %broadcast.203), dimensions={1}, to_apply=%all_to_all.26.reduce_sub_computation | reduce | bytes 2560004 | tf_op jit(solution)/shard_map/all_to_all | solution.py:53
  85.3 6.7 %reshape.219 = f32[640,5,2,50]{3,2,1,0:T(2,128)S(1)} reshape(f32[32,10000]{1,0:T(8,128)} %reduce) | data formatting | bytes 2560000
  92.0 2.8 %copy.20 = f32[32,5,2,50,20]{3,2,4,1,0:T(2,128)} copy(f32[32,5,2,50,20]{3,2,1,4,0:T(2,128)S(1)} %bitcast.42) | data formatting | bytes 2560000 | tf_op jit(solution)/shard_map/all_to_all | solution.py:53
  94.8 7.7 %copy.21 = f32[160,2,50,20]{0,1,2,3:T(2,128)} copy(f32[160,2,50,20]{2,1,3,0:T(2,128)} %bitcast.43) | data formatting | bytes 2560000 | tf_op jit(solution)/shard_map/all_to_all | solution.py:53
  102.5 0.0 copy-start.1
  102.5 5.2 %all-to-all-start.1 = ((f32[160,2,50,20]{0,1,2,3:T(2,128)}), f32[160,2,50,20]{0,1,2,3:T(2,128)}, u32[]{:S(2)}, u32[]{:S(2)}) async-start(f32[160,2,50,20]{0,1,2,3:T(2,128)} %copy.21), calls=%async_computation.1 | async-start | bytes 4096000 | tf_op jit(solution)/shard_map/all_to_all | solution.py:52
  107.6 0.0 copy-done.1
  107.6 0.2 reshape.184
  107.9 0.2 reshape.185
  108.1 15.2 %cosine_multiply_fusion = (f32[640,1,1280]{2,0,1:T(8,128)S(1)}, f32[640,1,1280]{2,0,1:T(8,128)}) fusion(s32[640]{0:T(1024)S(1)} %reshape.185, f32[640]{0:T(1024)S(1)} %get-tuple-element.24, f32[640]{0:T(1024)S(1)} %get-tuple-element.25), kind=kLoop, calls=%fused_computation.15 | loop fusion | flops 9011200 | bytes 6561280 | tf_op jit(solution)/shard_map/mul | solution.py:30
  123.3 10.4 %all-to-all-done.1 = f32[160,2,50,20]{0,1,2,3:T(2,128)} async-done(((f32[160,2,50,20]{0,1,2,3:T(2,128)}), f32[160,2,50,20]{0,1,2,3:T(2,128)}, u32[]{:S(2)}, u32[]{:S(2)}) %all-to-all-start.1) | async-done | bytes 1280032 | tf_op jit(solution)/shard_map/all_to_all | solution.py:52
  133.7 3.5 %copy.29 = f32[4,160,2,50,5]{1,0,3,2,4:T(4,128)} copy(f32[4,160,2,50,5]{1,2,3,4,0:T(2,128)} %bitcast.12) | data formatting | bytes 2560000 | tf_op jit(solution)/shard_map/all_to_all | solution.py:52
  137.1 3.6 %reshape.217 = f32[640,2,50,5]{0,2,1,3:T(8,128)} reshape(f32[4,160,2,50,5]{1,0,3,2,4:T(4,128)} %copy.29) | data formatting | bytes 2560000 | tf_op jit(solution)/shard_map/all_to_all | solution.py:52
  140.7 9.8 %fusion.10 = f32[5,50,1280]{2,1,0:T(8,128)} fusion(f32[640,2,50,5]{0,2,1,3:T(8,128)} %reshape.217, f32[640,1,1280]{2,0,1:T(8,128)} %get-tuple-element.23, f32[640,1,1280]{2,0,1:T(8,128)S(1)} %get-tuple-element.22), kind=kOutput, calls=%fused_computation.20 | convolution fusion | flops 4916838400 | bytes 9113600 | tf_op jit(solution)/shard_map/sreq,srl->qel/dot_general | solution.py:34
  (5 shorter events, 0.0 us)
Async XLA Ops:
  10.9 9.0 %copy-start = (f32[5,640,640]{2,1,0:T(8,128)S(1)}, f32[5,640,640]{2,1,0:T(8,128)}, u32[]{:S(2)}) copy-start(f32[5,640,640]{2,1,0:T(8,128)} %param.9) | copy-start | bytes 24576004
  102.5 5.2 %copy-start.1 = (s32[640]{0:T(1024)S(1)}, s32[640]{0:T(1024)}, u32[]{:S(2)}) copy-start(s32[640]{0:T(1024)} %param.12) | copy-start | bytes 7684
  102.5 31.2 %all-to-all-start.1 = ((f32[160,2,50,20]{0,1,2,3:T(2,128)}), f32[160,2,50,20]{0,1,2,3:T(2,128)}, u32[]{:S(2)}, u32[]{:S(2)}) async-start(f32[160,2,50,20]{0,1,2,3:T(2,128)} %copy.21), calls=%async_computation.1 | async-start | bytes 4096000 | tf_op jit(solution)/shard_map/all_to_all | solution.py:52
where the time goes:
time: 151 us; the launch traced here: 150 us
  local copies, waits for them, and re-layouts  50.1 us (33%)
  other arithmetic  36.4 us (24%)
  blocking collectives  28.6 us (19%)
  matrix products  19 us (13%)
  waiting for transfers between devices  10.4 us (7%)
  starting transfers between devices  5.16 us (3%)
    all_to_all x1, blocking collectives, local(): lax.all_to_all(field, 'lat', split_axis=3, concat_axis=0, tiled=True)  28.6 us
    mul x1, other arithmetic, synthesis_table(): weight * jnp.cos(angle)  15.2 us
    unnamed x6, local copies, waits for them, and re-layouts  13.2 us
    all_to_all x3, local copies, waits for them, and re-layouts, local(): lax.all_to_all(field, 'lat', split_axis=3, concat_axis=0, tiled=True)  11 us
    all_to_all x1, waiting for transfers between devices, local(): lax.all_to_all(lax.all_to_all(field, 'lat', split_axis=3, concat_axis=0,...  10.4 us
    dot_general x1, matrix products, synthesize(): jnp.einsum('sreq,srl->qel', values, table, precision=lax.Precision.HIGHEST)  9.76 us
    dot_general x1, matrix products, local(): jnp.einsum('srkej,slj->srel', coeffs_new, legendre, precision=lax.Precisi...  9.27 us
    reduce_sum x1, other arithmetic, local(): jnp.einsum('srkej,slj->srel', coeffs_new, legendre, precision=lax.Precisi...  9 us
  transfers between devices with their start and end apart: 1, of which 1 were waited for; matrix products, arithmetic and copies ran while one was open for 10% of the time, Pallas kernels for 0%

commit v1 on v0

v1 whole, which is shorter than its diff:
```python
import functools

import jax
import jax.numpy as jnp
from jax import lax
from jax.experimental import pallas as pl
from jax.experimental.pallas import tpu as pltpu
from jax.sharding import PartitionSpec as P

LON = 1280
TWO_PI = 6.283185307179586
AXES = ("lat", "lon")
F32 = jnp.float32
BF16 = jnp.bfloat16
LANES = 128


def split(x):
    high = x.astype(BF16)
    return high, (x - high.astype(F32)).astype(BF16)


def slot_factors(amp_ref, decay_ref, wave):
    scales, width = amp_ref.shape
    row = lax.broadcasted_iota(jnp.int32, (scales, width), 0)
    lane = lax.broadcasted_iota(jnp.int32, (scales, width), 1)
    decay = jnp.full((scales, width), decay_ref[0], F32)
    for k in range(1, scales):
        decay = jnp.where(row == k, decay_ref[k], decay)
    rolled = pltpu.roll(amp_ref[...], lax.rem(width - wave, width), 1)
    live = lane + wave < width
    zero = jnp.zeros((scales, width), F32)
    return (
        jnp.where(live, decay, zero),
        jnp.where(live, rolled * jnp.sqrt(1.0 - decay * decay), zero),
    )


def first_slot(slots):
    return (lax.axis_index("lat") * lax.axis_size("lon") + lax.axis_index("lon")) * slots


def field_kernel(
    waves_h, order_h, decay_h, amp_h, old_h, noise_h, leg_h, send_ref,
    waves, order, decay_ref, amp_ref, old_v, noise_v, leg_v, w_ref, f_ref, fac_ref, sems, small_sems,
):
    slots, scales, members, parts, width = old_h.shape
    lats = leg_h.shape[1]
    pairs = members * parts
    base = first_slot(slots)
    lane_tiles = f_ref.shape[0] // lats

    def copies(s, jt):
        cols = pl.ds(pl.multiple_of(jt * LANES, LANES), LANES)
        return (
            pltpu.make_async_copy(old_h.at[s, :, :, :, cols], old_v.at[s, :, :, :, cols], sems.at[s, jt, 0]),
            pltpu.make_async_copy(noise_h.at[s, :, :, :, cols], noise_v.at[s, :, :, :, cols], sems.at[s, jt, 1]),
            pltpu.make_async_copy(leg_h.at[s, :, cols], leg_v.at[s, :, cols], sems.at[s, jt, 2]),
        )

    small = [
        pltpu.make_async_copy(src, dst, small_sems.at[i])
        for i, (src, dst) in enumerate(
            ((waves_h, waves), (decay_h, decay_ref), (amp_h, amp_ref), (order_h, order))
        )
    ]
    for c in small:
        c.start()
    for s in range(slots):
        for c in copies(s, 0):
            c.start()
    f_ref[...] = jnp.zeros_like(f_ref)
    w_ref[...] = jnp.zeros_like(w_ref)
    for c in small[:3]:
        c.wait()
    counts = [(width - waves[base + s] + LANES - 1) // LANES for s in range(slots)]
    for s in range(slots):

        def start(jt, _, s=s):
            for c in copies(s, jt):
                c.start()
            return 0

        lax.fori_loop(1, counts[s], start, 0)
    for s in range(slots):
        decay, noise_factor = slot_factors(amp_ref, decay_ref, waves[base + s])
        fac_ref[s, 0] = decay
        fac_ref[s, 1] = noise_factor
    contract = (((1,), (1,)), ((), ()))
    for s in range(slots):
        tile, offset = divmod(s * pairs, LANES)
        wide = 2 if offset + pairs > LANES else 1

        def step(jt, _, s=s, tile=tile, offset=offset, wide=wide):
            cols = pl.ds(pl.multiple_of(jt * LANES, LANES), LANES)
            for c in copies(s, jt):
                c.wait()
            d = fac_ref[s, 0, :, cols]
            a = fac_ref[s, 1, :, cols]
            total = None
            for k in range(scales):
                term = d[k].reshape(1, 1, LANES) * old_v[s, k, :, :, cols] + a[k].reshape(1, 1, LANES) * noise_v[
                    s, k, :, :, cols
                ].astype(F32)
                total = term if total is None else total + term
            w_ref[s, offset : offset + pairs, :] = total.reshape(pairs, LANES)
            wh, wl = split(w_ref[s, : wide * LANES, :])
            lh, ll = split(leg_v[s, :, cols])
            res = lax.dot_general(
                jnp.concatenate([lh, ll], axis=1), jnp.concatenate([wh, wh], axis=1), contract,
                preferred_element_type=F32,
            ) + lax.dot_general(lh, wl, contract, preferred_element_type=F32)
            for w in range(wide):
                rows = pl.ds(tile + w, lats, stride=lane_tiles)
                f_ref[rows, :] = f_ref[rows, :] + res[:, w * LANES : (w + 1) * LANES]
            return 0

        lax.fori_loop(0, counts[s], step, 0)

    small[3].wait()
    f3 = f_ref.reshape(lats, lane_tiles, LANES)
    unroll = 8

    def gather(i, _):
        for u in range(unroll):
            q = i * unroll + u
            send_ref[q] = f3[order[q]]
        return 0

    lax.fori_loop(0, lats // unroll, gather, 0)


def evolve_kernel(waves, decay_ref, amp_ref, old_ref, noise_ref, new_ref, *, slots):
    scales = amp_ref.shape[0]
    d, a = slot_factors(amp_ref, decay_ref, waves[first_slot(slots) + pl.program_id(0)])
    for k in range(scales):
        new_ref[0, k] = d[k : k + 1][None] * old_ref[0, k] + a[k : k + 1][None] * noise_ref[0, k].astype(F32)


def trig(steps):
    turns = jnp.floor((steps + 0.5) * (1.0 / LON))
    rest = steps - turns * LON
    quarter = jnp.floor((rest + LON / 8) * (4.0 / LON))
    x = (rest - quarter * (LON / 4)) * (TWO_PI / LON)
    y = x * x
    sine = x * (1.0 + y * (-1.0 / 6 + y * (1.0 / 120 + y * (-1.0 / 5040 + y * (1.0 / 362880)))))
    cosine = 1.0 + y * (-0.5 + y * (1.0 / 24 + y * (-1.0 / 720 + y * (1.0 / 40320 - y * (1.0 / 3628800)))))
    odd = (quarter == 1.0) | (quarter == 3.0)
    c = jnp.where(odd, sine, cosine)
    s = jnp.where(odd, cosine, sine)
    c = jnp.where((quarter == 1.0) | (quarter == 2.0), -c, c)
    s = jnp.where((quarter == 2.0) | (quarter == 3.0), -s, s)
    return c, s


def table_kernel(wave_ref, high_ref, low_ref):
    count, slots = wave_ref.shape
    length = high_ref.shape[1]
    lane = lax.broadcasted_iota(jnp.int32, (count, LANES), 1)
    for s in range(slots):
        wave = jnp.broadcast_to(wave_ref[:, s : s + 1], (count, LANES))
        weight = jnp.where(wave == 0, 1.0, 2.0).astype(F32)
        c, n = trig((wave * lane).astype(F32))
        c1, n1 = trig((wave * LANES).astype(F32))
        c = c * weight
        n = -n * weight
        for b in range(length // LANES):
            cols = slice(b * LANES, (b + 1) * LANES)
            for r, value in enumerate((c, n)):
                rows = slice((2 * s + r) * count, (2 * s + r + 1) * count)
                high, low = split(value)
                high_ref[rows, cols] = high
                low_ref[rows, cols] = low
            c, n = c * c1 + n * n1, n * c1 - c * n1


def synthesis_kernel(recv_ref, high_ref, low_ref, out_ref, t_ref, x_ref, xx_ref, *, sources, slots):
    rows, members, block = out_ref.shape
    pitch = -(-members // 8) * 8
    tall = rows * pitch
    second = -(-tall // 16) * 16
    pairs = members * 2
    lane_tiles = recv_ref.shape[0] // (sources * rows)

    @pl.when(pl.program_id(0) == 0)
    def _():
        for q in range(rows):
            for t in range(lane_tiles):
                piece = recv_ref[pl.ds(q * lane_tiles + t, sources, stride=rows * lane_tiles), :]
                t_ref[q, t * LANES : (t + 1) * LANES, :] = piece.T
            for s in range(slots):
                for r in range(2):
                    g = 2 * s + r
                    x_ref[q * pitch : (q + 1) * pitch, g * sources : (g + 1) * sources] = t_ref[
                        q, pl.ds(s * pairs + r, pitch, stride=2), :
                    ]
        high, low = split(x_ref[...])
        xx_ref[0:tall, :] = high
        xx_ref[second : second + tall, :] = low

    both = jnp.dot(xx_ref[...], high_ref[...], preferred_element_type=F32)
    res = both[0:tall] + both[second : second + tall] + jnp.dot(
        xx_ref[0:tall, :], low_ref[...], preferred_element_type=F32
    )
    for q in range(rows):
        out_ref[q] = res[q * pitch : q * pitch + members]


def in_hbm(x):
    return pltpu.with_memory_space_constraint(x, pltpu.HBM)


def local(coeffs_old, noise, legendre, decay, amplitude, wavenumber_of_slot, lat_order):
    devices = lax.axis_size(AXES)
    slots, parts, scales, members, width = coeffs_old.shape
    lats = legendre.shape[1]
    rows = lats // devices
    waves = wavenumber_of_slot.astype(jnp.int32)
    order = lat_order.astype(jnp.int32)
    old = coeffs_old.transpose(0, 2, 3, 1, 4)
    fresh = noise.transpose(0, 2, 3, 1, 4)
    lane_tiles = -(-slots * parts * members // LANES)
    smem = pl.BlockSpec(memory_space=pltpu.SMEM)
    vmem = pl.BlockSpec(memory_space=pltpu.VMEM)
    hbm = pl.BlockSpec(memory_space=pltpu.HBM)

    with jax.named_scope("field"):
        send = pl.pallas_call(
            field_kernel,
            in_specs=[hbm] * 7,
            out_specs=vmem,
            out_shape=jax.ShapeDtypeStruct((lats, lane_tiles, LANES), F32),
            scratch_shapes=[
                pltpu.SMEM(waves.shape, jnp.int32),
                pltpu.SMEM(order.shape, jnp.int32),
                pltpu.SMEM(decay.shape, F32),
                pltpu.VMEM(amplitude.shape, F32),
                pltpu.VMEM((slots, scales, members, parts, width), F32),
                pltpu.VMEM((slots, scales, members, parts, width), BF16),
                pltpu.VMEM((slots, lats, width), F32),
                pltpu.VMEM((slots, 2 * LANES, LANES), F32),
                pltpu.VMEM((lats * lane_tiles, LANES), F32),
                pltpu.VMEM((slots, 2, scales, width), F32),
                pltpu.SemaphoreType.DMA((slots, width // LANES, 3)),
                pltpu.SemaphoreType.DMA((4,)),
            ],
            compiler_params=pltpu.CompilerParams(vmem_limit_bytes=40 << 20),
            cost_estimate=pl.CostEstimate(flops=10**9, transcendentals=0, bytes_accessed=14 * 10**6),
        )(*[in_hbm(x) for x in (waves, order, decay, amplitude, old, fresh, legendre)])

    with jax.named_scope("exchange"):
        recv = lax.all_to_all(send, AXES, split_axis=0, concat_axis=0, tiled=True)

    with jax.named_scope("evolve"):
        block = (1, scales, members, parts, width)
        new = pl.pallas_call(
            functools.partial(evolve_kernel, slots=slots),
            grid=(slots,),
            in_specs=[smem, smem, vmem] + [pl.BlockSpec(block, lambda i: (i, 0, 0, 0, 0))] * 2,
            out_specs=pl.BlockSpec(block, lambda i: (i, 0, 0, 0, 0)),
            out_shape=jax.ShapeDtypeStruct(old.shape, F32),
            compiler_params=pltpu.CompilerParams(vmem_limit_bytes=16 << 20),
            cost_estimate=pl.CostEstimate(flops=5 * 10**8, transcendentals=0, bytes_accessed=10**7),
        )(waves, decay, amplitude, old, fresh)
    coeffs_new = new.transpose(0, 3, 1, 2, 4)

    with jax.named_scope("table"):
        terms = devices * slots * parts
        high, low = pl.pallas_call(
            table_kernel,
            out_shape=[jax.ShapeDtypeStruct((terms, LON), BF16)] * 2,
            compiler_params=pltpu.CompilerParams(vmem_limit_bytes=24 << 20),
            cost_estimate=pl.CostEstimate(flops=5 * 10**8, transcendentals=0, bytes_accessed=7 * 10**6),
        )(waves.reshape(devices, slots))

    with jax.named_scope("synthesis"):
        cut = 256
        pitch = -(-members // 8) * 8
        tall = rows * pitch
        second = -(-tall // 16) * 16
        pattern = pl.pallas_call(
            functools.partial(synthesis_kernel, sources=devices, slots=slots),
            grid=(LON // cut,),
            in_specs=[vmem] + [pl.BlockSpec((terms, cut), lambda i: (0, i), memory_space=pltpu.VMEM)] * 2,
            out_specs=pl.BlockSpec((rows, members, cut), lambda i: (0, 0, i)),
            out_shape=jax.ShapeDtypeStruct((rows, members, LON), F32),
            scratch_shapes=[
                pltpu.VMEM((rows, lane_tiles * LANES, devices), F32),
                pltpu.VMEM((tall, terms), F32),
                pltpu.VMEM((2 * second, terms), BF16),
            ],
            compiler_params=pltpu.CompilerParams(vmem_limit_bytes=32 << 20),
        )(recv.reshape(lats * lane_tiles, LANES), in_hbm(high), in_hbm(low))
    return (coeffs_new, pattern)


def solution(mesh):
    split_first = P(AXES, None, None, None, None)
    in_specs = (split_first, split_first, P(AXES, None, None), P(), P(), P(), P())
    out_specs = (split_first, P(AXES, None, None))
    return jax.shard_map(local, mesh=mesh, in_specs=in_specs, out_specs=out_specs, check_vma=False)
```

time: 151 us -> 54.2 us (0.36)
  local copies, waits for them, and re-layouts: 50.1 us -> 5.69 us
  other arithmetic: 36.4 us -> 0 us
  Pallas kernels: 0 us -> 29.4 us
  blocking collectives: 28.6 us -> 0 us
  matrix products: 19 us -> 0 us
  starting transfers between devices: 5.16 us -> 11.5 us
  waiting for transfers between devices: 10.4 us -> 6.63 us
    pallas_call x0 -> x4, Pallas kernels: none -> 29.4 us  [the longest x1 11.8 us: local(): pl.pallas_call(field_kernel, in_specs=[hbm] * 7, out_specs=vmem, out_shap...]
    all_to_all x1 -> x0, blocking collectives: 28.6 us -> none  [local(): lax.all_to_all(field, 'lat', split_axis=3, concat_axis=0, tiled=True)]
    dot_general x2 -> x0, matrix products: 19 us -> none  [the longest x1 9.76 us: synthesize(): jnp.einsum('sreq,srl->qel', values, table, precision=lax.Precision.HIGHEST)]
    all_to_all x5 -> x0, local copies, waits for them, and re-layouts: 18 us -> none  [the longest x3 11 us: local(): lax.all_to_all(field, 'lat', split_axis=3, concat_axis=0, tiled=True)]
    mul x2 -> x0, other arithmetic: 15.3 us -> none  [the longest x1 15.2 us: synthesis_table(): weight * jnp.cos(angle)]
    gather x16 -> x0, local copies, waits for them, and re-layouts: 13.9 us -> none  [the longest x1 7.33 us: local(): field = jnp.take(field, lat_order, axis=3)]
    reduce_sum x1 -> x0, other arithmetic: 9 us -> none  [local(): jnp.einsum('srkej,slj->srel', coeffs_new, legendre, precision=lax.Precisi...]
    unnamed x6 -> x14, local copies, waits for them, and re-layouts: 13.2 us -> 5.5 us
  transfers between devices with their start and end apart: 1 -> 1, of which waited for: 1 -> 1; matrix products, arithmetic and copies ran while one was open for 10% -> 0% of each run, Pallas kernels for 0% -> 18%
where the time goes in v1:
time: 54.2 us; the launch traced here: 53.9 us
  Pallas kernels  29.4 us (54%)
  starting transfers between devices  11.5 us (21%)
  waiting for transfers between devices  6.63 us (12%)
  local copies, waits for them, and re-layouts  5.69 us (10%)
  between operations  0.74 us (1%)
    pallas_call x1, Pallas kernels, local(): pl.pallas_call(field_kernel, in_specs=[hbm] * 7, out_specs=vmem, out_shap...  11.8 us
    all_to_all x1, starting transfers between devices, local(): recv = lax.all_to_all(send, AXES, split_axis=0, concat_axis=0, tiled=True)  11.5 us
    pallas_call x1, Pallas kernels, local(): pl.pallas_call(functools.partial(synthesis_kernel, sources=devices, slots...  7.64 us
    pallas_call x1, Pallas kernels, local(): pl.pallas_call(functools.partial(evolve_kernel, slots=slots), grid=(slots...  7.04 us
    all_to_all x1, waiting for transfers between devices, local(): recv = lax.all_to_all(send, AXES, split_axis=0, concat_axis=0, tiled=True)  6.63 us
    unnamed x14, local copies, waits for them, and re-layouts  5.5 us
    pallas_call x1, Pallas kernels, local(): pl.pallas_call(table_kernel, out_shape=[jax.ShapeDtypeStruct((terms, LON)...  2.92 us
  transfers between devices with their start and end apart: 1, of which 1 were waited for; matrix products, arithmetic and copies ran while one was open for 0% of the time, Pallas kernels for 18%

profile of v1, /device:TPU:1, one launch (start us, length us, event | category | flops | bytes accessed | tf_op | source)
XLA Modules:
  0.0 53.9 jit_solution(15852875618172910307)
XLA Ops:
  0.6 0.0 copy-start.5
  0.6 0.0 copy-start.4
  0.7 0.0 copy-start.6
  0.7 11.8 %field.1 = f32[640,4,128]{2,1,0:T(4,128)} custom-call(s32[640]{0:T(1024)} %waves_h.1, s32[640]{0:T(1024)} %order_h.1, f32[3]{0:T(128)} %decay_h.1, f32[3,640]{1,0:T(4,128)} %amp_h.1, f32[5,3,50,2,640]{4,3,2,1,0:T(2,128)} %bitcast.4, bf16[5,3,50,2,640]{4,3,2,1,0:T(2,128)(2,1)} %bitcast.6, f32[5,640,640]{2,1,0:T(8,128)} %leg_h.1), custom_call_target="tpu_custom_call" | custom-call | flops 1000000000 | bytes 14000000 | tf_op jit(solution)/shard_map/field/pallas_call | solution.py:228
  12.4 0.0 copy-start.1
  12.4 11.5 %all-to-all-start = ((f32[640,4,128]{2,1,0:T(4,128)}), f32[640,4,128]{2,1,0:T(4,128)S(1)}, u32[]{:S(2)}, u32[]{:S(2)}) async-start(f32[640,4,128]{2,1,0:T(4,128)} %field.1), calls=%async_computation | async-start | bytes 2621440 | tf_op jit(solution)/shard_map/exchange/all_to_all | solution.py:252
  23.9 0.0 copy-done.5
  23.9 0.2 reshape.11.wave_ref
  24.1 0.0 copy-done.4
  24.2 0.0 copy-done.6
  24.2 0.0 copy-done.1
  24.2 0.0 copy-start
  24.2 2.1 %copy-done = f32[5,2,3,50,640]{4,1,3,2,0:T(2,128)S(1)} copy-done((f32[5,2,3,50,640]{4,1,3,2,0:T(2,128)S(1)}, f32[5,2,3,50,640]{4,1,3,2,0:T(2,128)}, u32[]{:S(2)}) %copy-start) | copy-done | bytes 3840024
  26.3 7.0 %evolve.1 = f32[5,3,50,2,640]{4,3,2,1,0:T(2,128)} custom-call(s32[640]{0:T(1024)S(1)} %copy-done.5, f32[3]{0:T(128)S(1)} %copy-done.6, f32[3,640]{1,0:T(4,128)S(1)} %copy-done.4, f32[5,3,50,2,640]{4,3,2,1,0:T(2,128)S(1)} %bitcast.5, bf16[5,3,50,2,640]{4,3,2,1,0:T(2,128)(2,1)S(1)} %bitcast.7), custom_call_target="tpu_custom_call" | custom-call | flops 500000000 | bytes 10000000 | tf_op jit(solution)/shard_map/evolve/pallas_call | solution.py:256
  33.3 2.9 %table.1 = (bf16[1280,1280]{1,0:T(8,128)(2,1)S(1)}, bf16[1280,1280]{1,0:T(8,128)(2,1)S(1)}) custom-call(s32[128,5]{1,0:T(8,128)S(1)} %reshape.11.wave_ref), custom_call_target="tpu_custom_call" | custom-call | flops 500000000 | bytes 7000000 | tf_op jit(solution)/shard_map/table/pallas_call | solution.py:269
  36.2 0.0 copy-start.2
  36.2 1.7 %copy-done.2 = bf16[1280,1280]{1,0:T(8,128)(2,1)} copy-done((bf16[1280,1280]{1,0:T(8,128)(2,1)}, bf16[1280,1280]{1,0:T(8,128)(2,1)S(1)}, u32[]{:S(2)}) %copy-start.2) | copy-done | bytes 3276824
  37.9 0.0 copy-start.3
  37.9 1.7 %copy-done.3 = bf16[1280,1280]{1,0:T(8,128)(2,1)} copy-done((bf16[1280,1280]{1,0:T(8,128)(2,1)}, bf16[1280,1280]{1,0:T(8,128)(2,1)S(1)}, u32[]{:S(2)}) %copy-start.3) | copy-done | bytes 3276824
  39.6 6.6 %all-to-all-done = f32[640,4,128]{2,1,0:T(4,128)S(1)} async-done(((f32[640,4,128]{2,1,0:T(4,128)}), f32[640,4,128]{2,1,0:T(4,128)S(1)}, u32[]{:S(2)}, u32[]{:S(2)}) %all-to-all-start) | async-done | bytes 1310752 | tf_op jit(solution)/shard_map/exchange/all_to_all | solution.py:252
  46.3 7.6 %synthesis.1 = f32[5,50,1280]{2,1,0:T(8,128)} custom-call(f32[2560,128]{1,0:T(8,128)S(1)} %bitcast.8, bf16[1280,1280]{1,0:T(8,128)(2,1)} %copy-done.2, bf16[1280,1280]{1,0:T(8,128)(2,1)} %copy-done.3), custom_call_target="tpu_custom_call" | custom-call | tf_op jit(solution)/shard_map/synthesis/pallas_call | solution.py:281
Async XLA Ops:
  0.6 23.3 %copy-start.5 = (s32[640]{0:T(1024)S(1)}, s32[640]{0:T(1024)}, u32[]{:S(2)}) copy-start(s32[640]{0:T(1024)} %waves_h.1) | copy-start | bytes 7684
  0.6 23.5 %copy-start.4 = (f32[3,640]{1,0:T(4,128)S(1)}, f32[3,640]{1,0:T(4,128)}, u32[]{:S(2)}) copy-start(f32[3,640]{1,0:T(4,128)} %amp_h.1) | copy-start | bytes 23044
  0.7 23.5 %copy-start.6 = (f32[3]{0:T(128)S(1)}, f32[3]{0:T(128)}, u32[]{:S(2)}) copy-start(f32[3]{0:T(128)} %decay_h.1) | copy-start | bytes 40
  12.4 11.7 %copy-start.1 = (bf16[5,2,3,50,640]{4,1,3,2,0:T(2,128)(2,1)S(1)}, bf16[5,2,3,50,640]{4,1,3,2,0:T(2,128)(2,1)}, u32[]{:S(2)}) copy-start(bf16[5,2,3,50,640]{4,1,3,2,0:T(2,128)(2,1)} %param.8) | copy-start | bytes 5760004
  12.4 33.8 %all-to-all-start = ((f32[640,4,128]{2,1,0:T(4,128)}), f32[640,4,128]{2,1,0:T(4,128)S(1)}, u32[]{:S(2)}, u32[]{:S(2)}) async-start(f32[640,4,128]{2,1,0:T(4,128)} %field.1), calls=%async_computation | async-start | bytes 2621440 | tf_op jit(solution)/shard_map/exchange/all_to_all | solution.py:252
  24.2 2.1 %copy-start = (f32[5,2,3,50,640]{4,1,3,2,0:T(2,128)S(1)}, f32[5,2,3,50,640]{4,1,3,2,0:T(2,128)}, u32[]{:S(2)}) copy-start(f32[5,2,3,50,640]{4,1,3,2,0:T(2,128)} %param.7) | copy-start | bytes 11520004
  36.2 1.7 %copy-start.2 = (bf16[1280,1280]{1,0:T(8,128)(2,1)}, bf16[1280,1280]{1,0:T(8,128)(2,1)S(1)}, u32[]{:S(2)}) copy-start(bf16[1280,1280]{1,0:T(8,128)(2,1)S(1)} %get-tuple-element.4.high_ref) | copy-start | bytes 9830404
  37.9 1.7 %copy-start.3 = (bf16[1280,1280]{1,0:T(8,128)(2,1)}, bf16[1280,1280]{1,0:T(8,128)(2,1)S(1)}, u32[]{:S(2)}) copy-start(bf16[1280,1280]{1,0:T(8,128)(2,1)S(1)} %get-tuple-element.5.low_ref) | copy-start | bytes 9830404

commit v2 on v0

v2 whole, which is shorter than its diff:
```python
import functools

import jax
import jax.numpy as jnp
from jax import lax
from jax.experimental import pallas as pl
from jax.experimental.pallas import tpu as pltpu
from jax.sharding import PartitionSpec as P

LON = 1280
TWO_PI = 6.283185307179586
AXES = ("lat", "lon")
F32 = jnp.float32
BF16 = jnp.bfloat16
LANES = 128


def split(x):
    high = x.astype(BF16)
    return high, (x - high.astype(F32)).astype(BF16)


def slot_factors(amp_ref, decay_ref, wave):
    scales, width = amp_ref.shape
    row = lax.broadcasted_iota(jnp.int32, (scales, width), 0)
    lane = lax.broadcasted_iota(jnp.int32, (scales, width), 1)
    decay = jnp.full((scales, width), decay_ref[0], F32)
    for k in range(1, scales):
        decay = jnp.where(row == k, decay_ref[k], decay)
    rolled = pltpu.roll(amp_ref[...], lax.rem(width - wave, width), 1)
    live = lane + wave < width
    zero = jnp.zeros((scales, width), F32)
    return (
        jnp.where(live, decay, zero),
        jnp.where(live, rolled * jnp.sqrt(1.0 - decay * decay), zero),
    )


def first_slot(slots):
    return (lax.axis_index("lat") * lax.axis_size("lon") + lax.axis_index("lon")) * slots


def field_kernel(
    waves_h, order_h, decay_h, amp_h, old_h, noise_h, leg_h, send_h,
    waves, order, decay_ref, amp_ref, old_v, noise_v, leg_v, w_ref, f_ref, fac_ref, list_ref, send_v,
    sems, small_sems, out_sems,
):
    slots, scales, members, parts, width = old_h.shape
    lats = leg_h.shape[1]
    pairs = members * parts
    base = first_slot(slots)
    lane_tiles = send_h.shape[1]
    tiles = width // LANES
    ring = sems.shape[0]
    old_p = old_v.reshape(old_v.shape[0], old_v.shape[1] // parts, parts, LANES)

    def place(i):
        s = list_ref[i] // tiles
        jt = lax.rem(list_ref[i], tiles)
        return s, jt, pl.ds(pl.multiple_of(jt * LANES, LANES), LANES)

    def copies(i):
        s, jt, cols = place(i)
        here = pl.ds((s * tiles + jt) * scales, scales)
        slot = lax.rem(i, ring)
        return (
            pltpu.make_async_copy(old_h.at[s, :, :, :, cols], old_p.at[here, 0:members], sems.at[slot, 0]),
            pltpu.make_async_copy(noise_h.at[s, :, :, :, cols], noise_v.at[here], sems.at[slot, 1]),
            pltpu.make_async_copy(leg_h.at[s, :, cols], leg_v.at[s, jt], sems.at[slot, 2]),
        )

    def begin(i):
        for c in copies(i):
            c.start()

    def arrive(i):
        for c in copies(i):
            c.wait()

    small = [
        pltpu.make_async_copy(src, dst, small_sems.at[i])
        for i, (src, dst) in enumerate(
            ((waves_h, waves), (decay_h, decay_ref), (amp_h, amp_ref), (order_h, order))
        )
    ]
    for c in small:
        c.start()
    for s in range(slots):
        list_ref[s] = s * tiles
    for i in range(min(ring, slots)):
        begin(i)
    f_ref[...] = jnp.zeros_like(f_ref)
    w_ref[...] = jnp.zeros_like(w_ref)
    for c in small[:3]:
        c.wait()
    live = slots
    for s in range(slots):
        count = (width - waves[base + s] + LANES - 1) // LANES

        def note(jt, live, s=s):
            list_ref[live] = s * tiles + jt
            return live + 1

        live = lax.fori_loop(1, count, note, live)
    for s in range(slots):
        decay, noise_factor = slot_factors(amp_ref, decay_ref, waves[base + s])
        fac_ref[s, 0] = decay
        fac_ref[s, 1] = noise_factor
    contract = (((1,), (1,)), ((), ()))

    group = 10

    def coefficients(i, buffer):
        s, jt, cols = place(i)
        d = fac_ref[s, 0, :, cols]
        a = fac_ref[s, 1, :, cols]
        at = (s * tiles + jt) * scales
        offset = lax.rem(s * pairs, LANES)
        for g in range(0, members, group):
            fresh = None
            for k in range(scales):
                term = a[k].reshape(1, 1, LANES) * noise_v[at + k, g : g + group].astype(F32)
                fresh = term if fresh is None else fresh + term
            total = fresh.reshape(group * parts, LANES)
            for k in range(scales):
                total = total + d[k : k + 1] * old_v[at + k, g * parts : (g + group) * parts]
            w_ref[buffer, s, pl.ds(offset + g * parts, group * parts), :] = total

    def product(i, buffer, scale):
        s, jt, cols = place(i)
        spread = w_ref.at[buffer, s]
        w = (spread[0:LANES, :] + spread[LANES : 2 * LANES, :]) * scale
        w = jnp.concatenate(split(w), axis=0)
        leg = jnp.concatenate(split(leg_v[s, jt]), axis=1)
        res = lax.dot_general(leg, jnp.concatenate([w, w], axis=1), contract, preferred_element_type=F32)
        rows = pl.ds(s, lats, stride=slots)
        f_ref[rows, :] = f_ref[rows, :] + (res[:, :LANES] + res[:, LANES:])

    unroll = 1
    last = live - 1
    for u in range(unroll):
        arrive(u)
        coefficients(u, u)

    def step(n, _):
        first = n * unroll
        for u in range(unroll):
            ahead = first + u + ring

            @pl.when((ahead >= min(ring, slots)) & (ahead < live))
            def _(ahead=ahead):
                begin(ahead)

        for u in range(unroll):
            coming = first + unroll + u

            @pl.when(coming < live)
            def _(coming=coming):
                arrive(coming)

        here = lax.rem(n, 2) * unroll
        there = unroll - here
        for u in range(unroll):
            i = first + u
            product(jnp.minimum(i, last), here + u, jnp.where(i < live, 1.0, 0.0).astype(F32))
        for u in range(unroll):
            coefficients(jnp.minimum(first + unroll + u, last), there + u)
        return 0

    lax.fori_loop(0, (live + unroll - 1) // unroll, step, 0)
    small[3].wait()
    row = lax.broadcasted_iota(jnp.int32, (lane_tiles, LANES), 0)
    lane = lax.broadcasted_iota(jnp.int32, (lane_tiles, LANES), 1)
    lower = row * LANES + lane < (row + 1) * pairs
    many = 32
    pieces = out_sems.shape[0]
    part = lats // pieces
    out = []
    for p in range(pieces):

        def gather(i, _, p=p):
            for u in range(many):
                q = p * part + i * many + u
                at = order[q] * slots
                send_v[q] = jnp.where(lower, f_ref[pl.ds(at, lane_tiles), :], f_ref[pl.ds(at + 1, lane_tiles), :])
            return 0

        lax.fori_loop(0, part // many, gather, 0)
        rows = pl.ds(p * part, part)
        out.append(pltpu.make_async_copy(send_v.at[rows], send_h.at[rows], out_sems.at[p]))
        out[-1].start()
    for c in out:
        c.wait()


def evolve_kernel(waves, decay_ref, amp_ref, old_ref, noise_ref, new_ref, *, slots):
    scales = amp_ref.shape[0]
    d, a = slot_factors(amp_ref, decay_ref, waves[first_slot(slots) + pl.program_id(0)])
    for k in range(scales):
        new_ref[0, k] = d[k : k + 1][None] * old_ref[0, k] + a[k : k + 1][None] * noise_ref[0, k].astype(F32)


def trig(steps):
    turns = jnp.floor((steps + 0.5) * (1.0 / LON))
    rest = steps - turns * LON
    quarter = jnp.floor((rest + LON / 8) * (4.0 / LON))
    x = (rest - quarter * (LON / 4)) * (TWO_PI / LON)
    y = x * x
    sine = x * (1.0 + y * (-1.0 / 6 + y * (1.0 / 120 + y * (-1.0 / 5040 + y * (1.0 / 362880)))))
    cosine = 1.0 + y * (-0.5 + y * (1.0 / 24 + y * (-1.0 / 720 + y * (1.0 / 40320))))
    odd = (quarter == 1.0) | (quarter == 3.0)
    c = jnp.where(odd, sine, cosine)
    s = jnp.where(odd, cosine, sine)
    c = jnp.where((quarter == 1.0) | (quarter == 2.0), -c, c)
    s = jnp.where((quarter == 2.0) | (quarter == 3.0), -s, s)
    return c, s


def synthesis_kernel(
    recv_ref, wave_ref, out_h, c_ref, n_ref, c1_ref, n1_ref, high_v, low_v, out_v, t_ref, x_ref, xx_ref, out_sems,
):
    sources, slots = wave_ref.shape
    blocks, terms, block = high_v.shape
    rows, members, _ = out_h.shape
    pitch = -(-members // 8) * 8
    tall = rows * pitch
    second = -(-tall // 16) * 16
    pairs = members * 2
    lane_tiles = recv_ref.shape[0] // (sources * rows)
    lane = lax.broadcasted_iota(jnp.int32, (sources, LANES), 1)
    leap_c, leap_s = trig((wave_ref[...] * LANES).astype(F32))
    for s in range(slots):
        wave = jnp.broadcast_to(wave_ref[:, s : s + 1], (sources, LANES))
        weight = jnp.where(wave == 0, 1.0, 2.0).astype(F32)
        c, n = trig((wave * lane).astype(F32))
        c_ref[s] = c * weight
        n_ref[s] = -n * weight
        c1_ref[s] = jnp.broadcast_to(leap_c[:, s : s + 1], (sources, LANES))
        n1_ref[s] = jnp.broadcast_to(leap_s[:, s : s + 1], (sources, LANES))
    for q in range(rows):
        for t in range(lane_tiles):
            piece = recv_ref[pl.ds(q * lane_tiles + t, sources, stride=rows * lane_tiles), :]
            t_ref[q, t * LANES : (t + 1) * LANES, :] = piece.T
        for s in range(slots):
            for r in range(2):
                g = 2 * s + r
                x_ref[q * pitch : (q + 1) * pitch, g * sources : (g + 1) * sources] = t_ref[
                    q, pl.ds(s * pairs + r, pitch, stride=2), :
                ]
    high, low = split(x_ref[...])
    xx_ref[0:tall, :] = high
    xx_ref[second : second + tall, :] = low

    def table(b):
        for s in range(slots):
            c, n, c1, n1 = c_ref[s], n_ref[s], c1_ref[s], n1_ref[s]
            for p in range(block // LANES):
                cols = slice(p * LANES, (p + 1) * LANES)
                for r, value in enumerate((c, n)):
                    at = slice((2 * s + r) * sources, (2 * s + r + 1) * sources)
                    high, low = split(value)
                    high_v[b, at, cols] = high
                    low_v[b, at, cols] = low
                c, n = c * c1 + n * n1, n * c1 - c * n1
            c_ref[s] = c
            n_ref[s] = n

    table(0)
    stores = []
    for b in range(blocks):
        both = jnp.dot(xx_ref[...], high_v[b], preferred_element_type=F32)
        res = both[0:tall] + both[second : second + tall] + jnp.dot(
            xx_ref[0:tall, :], low_v[b], preferred_element_type=F32
        )
        if b + 1 < blocks:
            table(b + 1)
        cols = pl.ds(b * block, block)
        for q in range(rows):
            out_v[q, :, cols] = res[q * pitch : q * pitch + members]
        store = pltpu.make_async_copy(out_v.at[:, :, cols], out_h.at[:, :, cols], out_sems.at[b])
        store.start()
        stores.append(store)
    for c in stores:
        c.wait()


def in_hbm(x):
    return pltpu.with_memory_space_constraint(x, pltpu.HBM)


def spec(space):
    return pl.BlockSpec(memory_space=space)


def run_field(waves, order, decay, amplitude, old, noise, legendre):
    slots, scales, members, parts, width = old.shape
    lats = legendre.shape[1]
    lane_tiles = -(-slots * parts * members // LANES)
    pitch = -(-parts * members // 16) * 16
    return pl.pallas_call(
        field_kernel,
        in_specs=[spec(pltpu.HBM)] * 7,
        out_specs=spec(pltpu.HBM),
        out_shape=pltpu.HBM((lats, lane_tiles, LANES), F32),
        scratch_shapes=[
            pltpu.SMEM(waves.shape, jnp.int32),
            pltpu.SMEM(order.shape, jnp.int32),
            pltpu.SMEM(decay.shape, F32),
            pltpu.VMEM(amplitude.shape, F32),
            pltpu.VMEM((slots * (width // LANES) * scales, pitch, LANES), F32),
            pltpu.VMEM((slots * (width // LANES) * scales, members, parts, LANES), BF16),
            pltpu.VMEM((slots, width // LANES, lats, LANES), F32),
            pltpu.VMEM((2 * 1, slots, 2 * LANES, LANES), F32),
            pltpu.VMEM((lats * slots, LANES), F32),
            pltpu.VMEM((slots, 2, scales, width), F32),
            pltpu.SMEM((slots * width // LANES,), jnp.int32),
            pltpu.VMEM((lats, lane_tiles, LANES), F32),
            pltpu.SemaphoreType.DMA((4, 3)),
            pltpu.SemaphoreType.DMA((4,)),
            pltpu.SemaphoreType.DMA((4,)),
        ],
        compiler_params=pltpu.CompilerParams(vmem_limit_bytes=40 << 20),
        cost_estimate=pl.CostEstimate(flops=10**9, transcendentals=0, bytes_accessed=14 * 10**6),
    )(*[in_hbm(x) for x in (waves, order, decay, amplitude, old, noise, legendre)])


def run_evolve(waves, decay, amplitude, old, noise):
    slots = old.shape[0]
    block = pl.BlockSpec((1,) + old.shape[1:], lambda i: (i, 0, 0, 0, 0))
    return pl.pallas_call(
        functools.partial(evolve_kernel, slots=slots),
        grid=(slots,),
        in_specs=[spec(pltpu.SMEM), spec(pltpu.SMEM), spec(pltpu.VMEM), block, block],
        out_specs=block,
        out_shape=jax.ShapeDtypeStruct(old.shape, F32),
        compiler_params=pltpu.CompilerParams(vmem_limit_bytes=16 << 20),
        cost_estimate=pl.CostEstimate(flops=5 * 10**8, transcendentals=0, bytes_accessed=10**7),
    )(waves, decay, amplitude, old, noise)


def run_synthesis(recv, wave_table, rows, members):
    sources, slots = wave_table.shape
    cut = 256
    blocks = LON // cut
    terms = sources * slots * 2
    tall = rows * (-(-members // 8) * 8)
    second = -(-tall // 16) * 16
    lane_tiles = recv.shape[0] // (sources * rows)
    return pl.pallas_call(
        synthesis_kernel,
        in_specs=[spec(pltpu.VMEM)] * 2,
        out_specs=spec(pltpu.HBM),
        out_shape=pltpu.HBM((rows, members, LON), F32),
        scratch_shapes=[pltpu.VMEM((slots, sources, LANES), F32)] * 4
        + [
            pltpu.VMEM((blocks, terms, cut), BF16),
            pltpu.VMEM((blocks, terms, cut), BF16),
            pltpu.VMEM((rows, members, LON), F32),
            pltpu.VMEM((rows, lane_tiles * LANES, sources), F32),
            pltpu.VMEM((tall, terms), F32),
            pltpu.VMEM((2 * second, terms), BF16),
            pltpu.SemaphoreType.DMA((blocks,)),
        ],
        compiler_params=pltpu.CompilerParams(vmem_limit_bytes=32 << 20),
    )(recv, wave_table)


def local(coeffs_old, noise, legendre, decay, amplitude, wavenumber_of_slot, lat_order):
    devices = lax.axis_size(AXES)
    slots, parts, scales, members, width = coeffs_old.shape
    lats = legendre.shape[1]
    waves = wavenumber_of_slot.astype(jnp.int32)
    order = lat_order.astype(jnp.int32)
    old = coeffs_old.transpose(0, 2, 3, 1, 4)
    fresh = noise.transpose(0, 2, 3, 1, 4)
    with jax.named_scope("field"):
        send = run_field(waves, order, decay, amplitude, old, fresh, legendre)
    with jax.named_scope("exchange"):
        recv = lax.all_to_all(send, AXES, split_axis=0, concat_axis=0, tiled=True)
    with jax.named_scope("evolve"):
        new = run_evolve(waves, decay, amplitude, old, fresh)
    with jax.named_scope("synthesis"):
        pattern = run_synthesis(recv.reshape(-1, LANES), waves.reshape(devices, slots), lats // devices, members)
    return (new.transpose(0, 3, 1, 2, 4), pattern)


def solution(mesh):
    split_first = P(AXES, None, None, None, None)
    in_specs = (split_first, split_first, P(AXES, None, None), P(), P(), P(), P())
    out_specs = (split_first, P(AXES, None, None))
    return jax.shard_map(local, mesh=mesh, in_specs=in_specs, out_specs=out_specs, check_vma=False)
```

time: 151 us -> 49.1 us (0.33)
  local copies, waits for them, and re-layouts: 50.1 us -> 2.3 us
  other arithmetic: 36.4 us -> 0 us
  blocking collectives: 28.6 us -> 0 us
  Pallas kernels: 0 us -> 21.4 us
  matrix products: 19 us -> 0 us
  starting transfers between devices: 5.16 us -> 11.5 us
  waiting for transfers between devices: 10.4 us -> 13 us
    all_to_all x1 -> x0, blocking collectives: 28.6 us -> none  [local(): lax.all_to_all(field, 'lat', split_axis=3, concat_axis=0, tiled=True)]
    pallas_call x0 -> x3, Pallas kernels: none -> 21.4 us  [the longest x1 9.12 us: run_field(): pl.pallas_call(field_kernel, in_specs=[spec(pltpu.HBM)] * 7, out_specs=sp...]
    dot_general x2 -> x0, matrix products: 19 us -> none  [the longest x1 9.76 us: synthesize(): jnp.einsum('sreq,srl->qel', values, table, precision=lax.Precision.HIGHEST)]
    all_to_all x5 -> x0, local copies, waits for them, and re-layouts: 18 us -> none  [the longest x3 11 us: local(): lax.all_to_all(field, 'lat', split_axis=3, concat_axis=0, tiled=True)]
    mul x2 -> x0, other arithmetic: 15.3 us -> none  [the longest x1 15.2 us: synthesis_table(): weight * jnp.cos(angle)]
    gather x16 -> x0, local copies, waits for them, and re-layouts: 13.9 us -> none  [the longest x1 7.33 us: local(): field = jnp.take(field, lat_order, axis=3)]
    unnamed x6 -> x10, local copies, waits for them, and re-layouts: 13.2 us -> 2.11 us
    reduce_sum x1 -> x0, other arithmetic: 9 us -> none  [local(): jnp.einsum('srkej,slj->srel', coeffs_new, legendre, precision=lax.Precisi...]
  transfers between devices with their start and end apart: 1 -> 1, of which waited for: 1 -> 1; matrix products, arithmetic and copies ran while one was open for 10% -> 0% of each run, Pallas kernels for 0% -> 14%
where the time goes in v2:
time: 49.1 us; the launch traced here: 48.9 us
  Pallas kernels  21.4 us (44%)
  waiting for transfers between devices  13 us (26%)
  starting transfers between devices  11.5 us (23%)
  local copies, waits for them, and re-layouts  2.3 us (5%)
  between operations  0.72 us (1%)
    all_to_all x1, waiting for transfers between devices, local(): recv = lax.all_to_all(send, AXES, split_axis=0, concat_axis=0, tiled=True)  13 us
    all_to_all x1, starting transfers between devices, local(): recv = lax.all_to_all(send, AXES, split_axis=0, concat_axis=0, tiled=True)  11.5 us
    pallas_call x1, Pallas kernels, run_field(): pl.pallas_call(field_kernel, in_specs=[spec(pltpu.HBM)] * 7, out_specs=sp...  9.12 us
    pallas_call x1, Pallas kernels, run_evolve(): pl.pallas_call(functools.partial(evolve_kernel, slots=slots), grid=(slots...  7.04 us
    pallas_call x1, Pallas kernels, run_synthesis(): pl.pallas_call(synthesis_kernel, in_specs=[spec(pltpu.VMEM)] * 2, out_spe...  5.21 us
    unnamed x10, local copies, waits for them, and re-layouts  2.11 us
  transfers between devices with their start and end apart: 1, of which 1 were waited for; matrix products, arithmetic and copies ran while one was open for 0% of the time, Pallas kernels for 14%

profile of v2, /device:TPU:1, one launch (start us, length us, event | category | flops | bytes accessed | tf_op | source)
XLA Modules:
  0.0 48.9 jit_solution(7154269734365905732)
XLA Ops:
  0.6 9.1 %field.1 = f32[640,4,128]{2,1,0:T(4,128)} custom-call(s32[640]{0:T(1024)} %waves_h.1, s32[640]{0:T(1024)} %order_h.1, f32[3]{0:T(128)} %decay_h.1, f32[3,640]{1,0:T(4,128)} %amp_h.1, f32[5,3,50,2,640]{4,3,2,1,0:T(2,128)} %bitcast.4, bf16[5,3,50,2,640]{4,3,2,1,0:T(2,128)(2,1)} %bitcast.6, f32[5,640,640]{2,1,0:T(8,128)} %leg_h.1), custom_call_target="tpu_custom_call" | custom-call | flops 1000000000 | bytes 14000000 | tf_op jit(solution)/shard_map/field/pallas_call | solution.py:300
  9.8 0.0 copy-start.3
  9.8 0.0 copy-start.1
  9.8 0.0 copy-start.2
  9.8 0.0 copy-start.4
  9.8 11.5 %all-to-all-start = ((f32[640,4,128]{2,1,0:T(4,128)}), f32[640,4,128]{2,1,0:T(4,128)S(1)}, u32[]{:S(2)}, u32[]{:S(2)}) async-start(f32[640,4,128]{2,1,0:T(4,128)} %field.1), calls=%async_computation | async-start | bytes 2621440 | tf_op jit(solution)/shard_map/exchange/all_to_all | solution.py:379
  21.3 0.0 copy-done.3
  21.3 0.2 reshape.11.wave_ref
  21.5 0.0 copy-done.1
  21.5 0.0 copy-done.2
  21.5 0.0 copy-done.4
  21.6 0.0 copy-start
  21.6 2.1 %copy-done = f32[5,2,3,50,640]{4,1,3,2,0:T(2,128)S(1)} copy-done((f32[5,2,3,50,640]{4,1,3,2,0:T(2,128)S(1)}, f32[5,2,3,50,640]{4,1,3,2,0:T(2,128)}, u32[]{:S(2)}) %copy-start) | copy-done | bytes 3840024
  23.6 7.0 %evolve.1 = f32[5,3,50,2,640]{4,3,2,1,0:T(2,128)} custom-call(s32[640]{0:T(1024)S(1)} %copy-done.3, f32[3]{0:T(128)S(1)} %copy-done.4, f32[3,640]{1,0:T(4,128)S(1)} %copy-done.2, f32[5,3,50,2,640]{4,3,2,1,0:T(2,128)S(1)} %bitcast.5, bf16[5,3,50,2,640]{4,3,2,1,0:T(2,128)(2,1)S(1)} %bitcast.7), custom_call_target="tpu_custom_call" | custom-call | flops 500000000 | bytes 10000000 | tf_op jit(solution)/shard_map/evolve/pallas_call | solution.py:330
  30.7 13.0 %all-to-all-done = f32[640,4,128]{2,1,0:T(4,128)S(1)} async-done(((f32[640,4,128]{2,1,0:T(4,128)}), f32[640,4,128]{2,1,0:T(4,128)S(1)}, u32[]{:S(2)}, u32[]{:S(2)}) %all-to-all-start) | async-done | bytes 1310752 | tf_op jit(solution)/shard_map/exchange/all_to_all | solution.py:379
  43.7 5.2 %synthesis.1 = f32[5,50,1280]{2,1,0:T(8,128)} custom-call(f32[2560,128]{1,0:T(8,128)S(1)} %bitcast.8, s32[128,5]{1,0:T(8,128)S(1)} %reshape.11.wave_ref), custom_call_target="tpu_custom_call" | custom-call | tf_op jit(solution)/shard_map/synthesis/pallas_call | solution.py:349
Async XLA Ops:
  9.8 11.6 %copy-start.3 = (s32[640]{0:T(1024)S(1)}, s32[640]{0:T(1024)}, u32[]{:S(2)}) copy-start(s32[640]{0:T(1024)} %waves_h.1) | copy-start | bytes 7684
  9.8 11.8 %copy-start.1 = (bf16[5,2,3,50,640]{4,1,3,2,0:T(2,128)(2,1)S(1)}, bf16[5,2,3,50,640]{4,1,3,2,0:T(2,128)(2,1)}, u32[]{:S(2)}) copy-start(bf16[5,2,3,50,640]{4,1,3,2,0:T(2,128)(2,1)} %param.8) | copy-start | bytes 5760004
  9.8 11.8 %copy-start.2 = (f32[3,640]{1,0:T(4,128)S(1)}, f32[3,640]{1,0:T(4,128)}, u32[]{:S(2)}) copy-start(f32[3,640]{1,0:T(4,128)} %amp_h.1) | copy-start | bytes 23044
  9.8 11.8 %copy-start.4 = (f32[3]{0:T(128)S(1)}, f32[3]{0:T(128)}, u32[]{:S(2)}) copy-start(f32[3]{0:T(128)} %decay_h.1) | copy-start | bytes 40
  9.8 33.9 %all-to-all-start = ((f32[640,4,128]{2,1,0:T(4,128)}), f32[640,4,128]{2,1,0:T(4,128)S(1)}, u32[]{:S(2)}, u32[]{:S(2)}) async-start(f32[640,4,128]{2,1,0:T(4,128)} %field.1), calls=%async_computation | async-start | bytes 2621440 | tf_op jit(solution)/shard_map/exchange/all_to_all | solution.py:379
  21.6 2.1 %copy-start = (f32[5,2,3,50,640]{4,1,3,2,0:T(2,128)S(1)}, f32[5,2,3,50,640]{4,1,3,2,0:T(2,128)}, u32[]{:S(2)}) copy-start(f32[5,2,3,50,640]{4,1,3,2,0:T(2,128)} %param.7) | copy-start | bytes 11520004

commit v3 on v2

--- a/solution.py
+++ b/solution.py
@@ -55,8 +55,8 @@
     old_p = old_v.reshape(old_v.shape[0], old_v.shape[1] // parts, parts, LANES)
 
     def place(i):
-        s = list_ref[i] // tiles
-        jt = lax.rem(list_ref[i], tiles)
+        s = list_ref[0, i]
+        jt = list_ref[1, i]
         return s, jt, pl.ds(pl.multiple_of(jt * LANES, LANES), LANES)
 
     def copies(i):
@@ -86,7 +86,8 @@
     for c in small:
         c.start()
     for s in range(slots):
-        list_ref[s] = s * tiles
+        list_ref[0, s] = s
+        list_ref[1, s] = 0
     for i in range(min(ring, slots)):
         begin(i)
     f_ref[...] = jnp.zeros_like(f_ref)
@@ -98,7 +99,8 @@
         count = (width - waves[base + s] + LANES - 1) // LANES
 
         def note(jt, live, s=s):
-            list_ref[live] = s * tiles + jt
+            list_ref[0, live] = s
+            list_ref[1, live] = jt
             return live + 1
 
         live = lax.fori_loop(1, count, note, live)
@@ -116,15 +118,19 @@
         a = fac_ref[s, 1, :, cols]
         at = (s * tiles + jt) * scales
         offset = lax.rem(s * pairs, LANES)
+        target = w_ref.at[buffer, s]
         for g in range(0, members, group):
             fresh = None
             for k in range(scales):
                 term = a[k].reshape(1, 1, LANES) * noise_v[at + k, g : g + group].astype(F32)
                 fresh = term if fresh is None else fresh + term
-            total = fresh.reshape(group * parts, LANES)
-            for k in range(scales):
-                total = total + d[k : k + 1] * old_v[at + k, g * parts : (g + group) * parts]
-            w_ref[buffer, s, pl.ds(offset + g * parts, group * parts), :] = total
+            for e in range(group):
+                target[pl.ds(offset + (g + e) * parts, parts), :] = fresh[e]
+        rows = pl.ds(offset, pairs)
+        total = target[rows, :]
+        for k in range(scales):
+            total = total + d[k : k + 1] * old_v[at + k, 0:pairs]
+        target[rows, :] = total
 
     def product(i, buffer, scale):
         s, jt, cols = place(i)
@@ -217,15 +223,17 @@
 
 
 def synthesis_kernel(
-    recv_ref, wave_ref, out_h, c_ref, n_ref, c1_ref, n1_ref, high_v, low_v, out_v, t_ref, x_ref, xx_ref, out_sems,
+    recv_ref, wave_ref, out_h, c_ref, n_ref, c1_ref, n1_ref, high_v, low_v, out_v, t_ref, x_ref, xx_ref, g_ref, out_sems,
 ):
     sources, slots = wave_ref.shape
-    blocks, terms, block = high_v.shape
-    rows, members, _ = out_h.shape
+    blocks, kinds, _, block = high_v.shape
+    rows, members, length = out_h.shape
     pitch = -(-members // 8) * 8
     tall = rows * pitch
     second = -(-tall // 16) * 16
     pairs = members * 2
+    half = length // 2
+    tiles = half // LANES
     lane_tiles = recv_ref.shape[0] // (sources * rows)
     lane = lax.broadcasted_iota(jnp.int32, (sources, LANES), 1)
     leap_c, leap_s = trig((wave_ref[...] * LANES).astype(F32))
@@ -242,14 +250,14 @@
             piece = recv_ref[pl.ds(q * lane_tiles + t, sources, stride=rows * lane_tiles), :]
             t_ref[q, t * LANES : (t + 1) * LANES, :] = piece.T
         for s in range(slots):
-            for r in range(2):
-                g = 2 * s + r
-                x_ref[q * pitch : (q + 1) * pitch, g * sources : (g + 1) * sources] = t_ref[
+            for r in range(kinds):
+                x_ref[r, q * pitch : (q + 1) * pitch, s * sources : (s + 1) * sources] = t_ref[
                     q, pl.ds(s * pairs + r, pitch, stride=2), :
                 ]
-    high, low = split(x_ref[...])
-    xx_ref[0:tall, :] = high
-    xx_ref[second : second + tall, :] = low
+    for r in range(kinds):
+        high, low = split(x_ref[r])
+        xx_ref[r, 0:tall, :] = high
+        xx_ref[r, second : second + tall, :] = low
 
     def table(b):
         for s in range(slots):
@@ -257,29 +265,50 @@
             for p in range(block // LANES):
                 cols = slice(p * LANES, (p + 1) * LANES)
                 for r, value in enumerate((c, n)):
-                    at = slice((2 * s + r) * sources, (2 * s + r + 1) * sources)
+                    at = slice(s * sources, (s + 1) * sources)
                     high, low = split(value)
-                    high_v[b, at, cols] = high
-                    low_v[b, at, cols] = low
+                    high_v[b, r, at, cols] = high
+                    low_v[b, r, at, cols] = low
                 c, n = c * c1 + n * n1, n * c1 - c * n1
             c_ref[s] = c
             n_ref[s] = n
 
+    def summed(b, r):
+        both = jnp.dot(xx_ref[r], high_v[b, r], preferred_element_type=F32)
+        return both[0:tall] + both[second : second + tall] + jnp.dot(
+            xx_ref[r, 0:tall, :], low_v[b, r], preferred_element_type=F32
+        )
+
+    def leave(first, size, index):
+        cols = pl.ds(first, size)
+        return pltpu.make_async_copy(out_v.at[:, :, cols], out_h.at[:, :, cols], out_sems.at[index])
+
     table(0)
+    column = lax.broadcasted_iota(jnp.int32, (tall, LANES), 1)
+    mirror = lax.rem(LANES - column, LANES)
     stores = []
     for b in range(blocks):
-        both = jnp.dot(xx_ref[...], high_v[b], preferred_element_type=F32)
-        res = both[0:tall] + both[second : second + tall] + jnp.dot(
-            xx_ref[0:tall, :], low_v[b], preferred_element_type=F32
-        )
+        even = summed(b, 0)
+        odd = summed(b, 1)
         if b + 1 < blocks:
             table(b + 1)
-        cols = pl.ds(b * block, block)
+        width = min(block, half - b * block)
+        forward = even + odd
         for q in range(rows):
-            out_v[q, :, cols] = res[q * pitch : q * pitch + members]
-        store = pltpu.make_async_copy(out_v.at[:, :, cols], out_h.at[:, :, cols], out_sems.at[b])
-        store.start()
-        stores.append(store)
+            out_v[q, :, b * block : b * block + width] = forward[q * pitch : q * pitch + members, :width]
+        g_ref[:, b * block : (b + 1) * block] = even - odd
+        stores.append(leave(b * block, width, len(stores)))
+        stores[-1].start()
+        lowest = b * (block // LANES) - 1
+        done = [t for t in range(lowest, lowest + block // LANES) if 0 <= t < tiles]
+        for t in done:
+            back = jnp.take_along_axis(g_ref[:, t * LANES : (t + 1) * LANES], mirror, axis=1)
+            back = jnp.where(column == 0, g_ref[:, (t + 1) * LANES : (t + 2) * LANES], back)
+            at = length - (t + 1) * LANES
+            for q in range(rows):
+                out_v[q, :, at : at + LANES] = back[q * pitch : q * pitch + members]
+        stores.append(leave(length - (done[-1] + 1) * LANES, len(done) * LANES, len(stores)))
+        stores[-1].start()
     for c in stores:
         c.wait()
 
@@ -313,7 +342,7 @@
             pltpu.VMEM((2 * 1, slots, 2 * LANES, LANES), F32),
             pltpu.VMEM((lats * slots, LANES), F32),
             pltpu.VMEM((slots, 2, scales, width), F32),
-            pltpu.SMEM((slots * width // LANES,), jnp.int32),
+            pltpu.SMEM((2, slots * width // LANES), jnp.int32),
             pltpu.VMEM((lats, lane_tiles, LANES), F32),
             pltpu.SemaphoreType.DMA((4, 3)),
             pltpu.SemaphoreType.DMA((4,)),
@@ -341,8 +370,8 @@
 def run_synthesis(recv, wave_table, rows, members):
     sources, slots = wave_table.shape
     cut = 256
-    blocks = LON // cut
-    terms = sources * slots * 2
+    blocks = LON // 2 // cut + 1
+    terms = sources * slots
     tall = rows * (-(-members // 8) * 8)
     second = -(-tall // 16) * 16
     lane_tiles = recv.shape[0] // (sources * rows)
@@ -353,13 +382,14 @@
         out_shape=pltpu.HBM((rows, members, LON), F32),
         scratch_shapes=[pltpu.VMEM((slots, sources, LANES), F32)] * 4
         + [
-            pltpu.VMEM((blocks, terms, cut), BF16),
-            pltpu.VMEM((blocks, terms, cut), BF16),
+            pltpu.VMEM((blocks, 2, terms, cut), BF16),
+            pltpu.VMEM((blocks, 2, terms, cut), BF16),
             pltpu.VMEM((rows, members, LON), F32),
             pltpu.VMEM((rows, lane_tiles * LANES, sources), F32),
-            pltpu.VMEM((tall, terms), F32),
-            pltpu.VMEM((2 * second, terms), BF16),
-            pltpu.SemaphoreType.DMA((blocks,)),
+            pltpu.VMEM((2, tall, terms), F32),
+            pltpu.VMEM((2, 2 * second, terms), BF16),
+            pltpu.VMEM((tall, blocks * cut), F32),
+            pltpu.SemaphoreType.DMA((2 * blocks,)),
         ],
         compiler_params=pltpu.CompilerParams(vmem_limit_bytes=32 << 20),
     )(recv, wave_table)

time: 49.1 us -> 47.6 us (0.969)
  Pallas kernels: 21.4 us -> 19.8 us
    pallas_call x1, Pallas kernels: 5.21 us -> 4.25 us  [run_synthesis(): pl.pallas_call(synthesis_kernel, in_specs=[spec(pltpu.VMEM)] * 2, out_spe...]
    pallas_call x1, Pallas kernels: 9.12 us -> 8.56 us  [run_field(): pl.pallas_call(field_kernel, in_specs=[spec(pltpu.HBM)] * 7, out_specs=sp...]
  transfers between devices with their start and end apart: 1 -> 1, of which waited for: 1 -> 1; matrix products, arithmetic and copies ran while one was open for 0% -> 0% of each run, Pallas kernels for 14% -> 15%
where the time goes in v3:
time: 47.6 us; the launch traced here: 47.3 us
  Pallas kernels  19.8 us (42%)
  waiting for transfers between devices  13 us (27%)
  starting transfers between devices  11.5 us (24%)
  local copies, waits for them, and re-layouts  2.3 us (5%)
  between operations  0.72 us (2%)
    all_to_all x1, waiting for transfers between devices, local(): recv = lax.all_to_all(send, AXES, split_axis=0, concat_axis=0, tiled=True)  13 us
    all_to_all x1, starting transfers between devices, local(): recv = lax.all_to_all(send, AXES, split_axis=0, concat_axis=0, tiled=True)  11.5 us
    pallas_call x1, Pallas kernels, run_field(): pl.pallas_call(field_kernel, in_specs=[spec(pltpu.HBM)] * 7, out_specs=sp...  8.56 us
    pallas_call x1, Pallas kernels, run_evolve(): pl.pallas_call(functools.partial(evolve_kernel, slots=slots), grid=(slots...  7.04 us
    pallas_call x1, Pallas kernels, run_synthesis(): pl.pallas_call(synthesis_kernel, in_specs=[spec(pltpu.VMEM)] * 2, out_spe...  4.25 us
    unnamed x10, local copies, waits for them, and re-layouts  2.11 us
  transfers between devices with their start and end apart: 1, of which 1 were waited for; matrix products, arithmetic and copies ran while one was open for 0% of the time, Pallas kernels for 15%

profile of v3, /device:TPU:1, one launch (start us, length us, event | category | flops | bytes accessed | tf_op | source)
XLA Modules:
  0.0 47.3 jit_solution(5496190262048528297)
XLA Ops:
  0.6 8.6 %field.1 = f32[640,4,128]{2,1,0:T(4,128)} custom-call(s32[640]{0:T(1024)} %waves_h.1, s32[640]{0:T(1024)} %order_h.1, f32[3]{0:T(128)} %decay_h.1, f32[3,640]{1,0:T(4,128)} %amp_h.1, f32[5,3,50,2,640]{4,3,2,1,0:T(2,128)} %bitcast.4, bf16[5,3,50,2,640]{4,3,2,1,0:T(2,128)(2,1)} %bitcast.6, f32[5,640,640]{2,1,0:T(8,128)} %leg_h.1), custom_call_target="tpu_custom_call" | custom-call | flops 1000000000 | bytes 14000000 | tf_op jit(solution)/shard_map/field/pallas_call | solution.py:329
  9.2 0.0 copy-start.3
  9.2 0.0 copy-start.1
  9.2 0.0 copy-start.2
  9.2 0.0 copy-start.4
  9.2 11.5 %all-to-all-start = ((f32[640,4,128]{2,1,0:T(4,128)}), f32[640,4,128]{2,1,0:T(4,128)S(1)}, u32[]{:S(2)}, u32[]{:S(2)}) async-start(f32[640,4,128]{2,1,0:T(4,128)} %field.1), calls=%async_computation | async-start | bytes 2621440 | tf_op jit(solution)/shard_map/exchange/all_to_all | solution.py:409
  20.7 0.0 copy-done.3
  20.7 0.2 reshape.11.wave_ref
  20.9 0.0 copy-done.1
  21.0 0.0 copy-done.2
  21.0 0.0 copy-done.4
  21.0 0.0 copy-start
  21.0 2.1 %copy-done = f32[5,2,3,50,640]{4,1,3,2,0:T(2,128)S(1)} copy-done((f32[5,2,3,50,640]{4,1,3,2,0:T(2,128)S(1)}, f32[5,2,3,50,640]{4,1,3,2,0:T(2,128)}, u32[]{:S(2)}) %copy-start) | copy-done | bytes 3840024
  23.1 7.0 %evolve.1 = f32[5,3,50,2,640]{4,3,2,1,0:T(2,128)} custom-call(s32[640]{0:T(1024)S(1)} %copy-done.3, f32[3]{0:T(128)S(1)} %copy-done.4, f32[3,640]{1,0:T(4,128)S(1)} %copy-done.2, f32[5,3,50,2,640]{4,3,2,1,0:T(2,128)S(1)} %bitcast.5, bf16[5,3,50,2,640]{4,3,2,1,0:T(2,128)(2,1)S(1)} %bitcast.7), custom_call_target="tpu_custom_call" | custom-call | flops 500000000 | bytes 10000000 | tf_op jit(solution)/shard_map/evolve/pallas_call | solution.py:359
  30.1 13.0 %all-to-all-done = f32[640,4,128]{2,1,0:T(4,128)S(1)} async-done(((f32[640,4,128]{2,1,0:T(4,128)}), f32[640,4,128]{2,1,0:T(4,128)S(1)}, u32[]{:S(2)}, u32[]{:S(2)}) %all-to-all-start) | async-done | bytes 1310752 | tf_op jit(solution)/shard_map/exchange/all_to_all | solution.py:409
  43.1 4.2 %synthesis.1 = f32[5,50,1280]{2,1,0:T(8,128)} custom-call(f32[2560,128]{1,0:T(8,128)S(1)} %bitcast.8, s32[128,5]{1,0:T(8,128)S(1)} %reshape.11.wave_ref), custom_call_target="tpu_custom_call" | custom-call | tf_op jit(solution)/shard_map/synthesis/pallas_call | solution.py:378
Async XLA Ops:
  9.2 11.5 %copy-start.3 = (s32[640]{0:T(1024)S(1)}, s32[640]{0:T(1024)}, u32[]{:S(2)}) copy-start(s32[640]{0:T(1024)} %waves_h.1) | copy-start | bytes 7684
  9.2 11.7 %copy-start.1 = (bf16[5,2,3,50,640]{4,1,3,2,0:T(2,128)(2,1)S(1)}, bf16[5,2,3,50,640]{4,1,3,2,0:T(2,128)(2,1)}, u32[]{:S(2)}) copy-start(bf16[5,2,3,50,640]{4,1,3,2,0:T(2,128)(2,1)} %param.8) | copy-start | bytes 5760004
  9.2 11.7 %copy-start.2 = (f32[3,640]{1,0:T(4,128)S(1)}, f32[3,640]{1,0:T(4,128)}, u32[]{:S(2)}) copy-start(f32[3,640]{1,0:T(4,128)} %amp_h.1) | copy-start | bytes 23044
  9.2 11.7 %copy-start.4 = (f32[3]{0:T(128)S(1)}, f32[3]{0:T(128)}, u32[]{:S(2)}) copy-start(f32[3]{0:T(128)} %decay_h.1) | copy-start | bytes 40
  9.2 33.8 %all-to-all-start = ((f32[640,4,128]{2,1,0:T(4,128)}), f32[640,4,128]{2,1,0:T(4,128)S(1)}, u32[]{:S(2)}, u32[]{:S(2)}) async-start(f32[640,4,128]{2,1,0:T(4,128)} %field.1), calls=%async_computation | async-start | bytes 2621440 | tf_op jit(solution)/shard_map/exchange/all_to_all | solution.py:409
  21.0 2.1 %copy-start = (f32[5,2,3,50,640]{4,1,3,2,0:T(2,128)S(1)}, f32[5,2,3,50,640]{4,1,3,2,0:T(2,128)}, u32[]{:S(2)}) copy-start(f32[5,2,3,50,640]{4,1,3,2,0:T(2,128)} %param.7) | copy-start | bytes 11520004

commit v4 on v3

--- a/solution.py
+++ b/solution.py
@@ -62,7 +62,7 @@
     def copies(i):
         s, jt, cols = place(i)
         here = pl.ds((s * tiles + jt) * scales, scales)
-        slot = lax.rem(i, ring)
+        slot = i & (ring - 1)
         return (
             pltpu.make_async_copy(old_h.at[s, :, :, :, cols], old_p.at[here, 0:members], sems.at[slot, 0]),
             pltpu.make_async_copy(noise_h.at[s, :, :, :, cols], noise_v.at[here], sems.at[slot, 1]),
@@ -117,7 +117,7 @@
         d = fac_ref[s, 0, :, cols]
         a = fac_ref[s, 1, :, cols]
         at = (s * tiles + jt) * scales
-        offset = lax.rem(s * pairs, LANES)
+        offset = (s * pairs) & (LANES - 1)
         target = w_ref.at[buffer, s]
         for g in range(0, members, group):
             fresh = None
@@ -164,7 +164,7 @@
             def _(coming=coming):
                 arrive(coming)
 
-        here = lax.rem(n, 2) * unroll
+        here = (n & 1) * unroll
         there = unroll - here
         for u in range(unroll):
             i = first + u
@@ -178,7 +178,7 @@
     row = lax.broadcasted_iota(jnp.int32, (lane_tiles, LANES), 0)
     lane = lax.broadcasted_iota(jnp.int32, (lane_tiles, LANES), 1)
     lower = row * LANES + lane < (row + 1) * pairs
-    many = 32
+    many = 128
     pieces = out_sems.shape[0]
     part = lats // pieces
     out = []
@@ -346,7 +346,7 @@
             pltpu.VMEM((lats, lane_tiles, LANES), F32),
             pltpu.SemaphoreType.DMA((4, 3)),
             pltpu.SemaphoreType.DMA((4,)),
-            pltpu.SemaphoreType.DMA((4,)),
+            pltpu.SemaphoreType.DMA((5,)),
         ],
         compiler_params=pltpu.CompilerParams(vmem_limit_bytes=40 << 20),
         cost_estimate=pl.CostEstimate(flops=10**9, transcendentals=0, bytes_accessed=14 * 10**6),

time: 47.6 us -> 47.5 us (level)
  no operation moved by 1% of the time
where the time goes in v4:
time: 47.5 us; the launch traced here: 47.2 us
  Pallas kernels  19.7 us (41%)
  waiting for transfers between devices  13 us (27%)
  starting transfers between devices  11.5 us (24%)
  local copies, waits for them, and re-layouts  2.3 us (5%)
  between operations  0.72 us (2%)
    all_to_all x1, waiting for transfers between devices, local(): recv = lax.all_to_all(send, AXES, split_axis=0, concat_axis=0, tiled=True)  13 us
    all_to_all x1, starting transfers between devices, local(): recv = lax.all_to_all(send, AXES, split_axis=0, concat_axis=0, tiled=True)  11.5 us
    pallas_call x1, Pallas kernels, run_field(): pl.pallas_call(field_kernel, in_specs=[spec(pltpu.HBM)] * 7, out_specs=sp...  8.39 us
    pallas_call x1, Pallas kernels, run_evolve(): pl.pallas_call(functools.partial(evolve_kernel, slots=slots), grid=(slots...  7.04 us
    pallas_call x1, Pallas kernels, run_synthesis(): pl.pallas_call(synthesis_kernel, in_specs=[spec(pltpu.VMEM)] * 2, out_spe...  4.25 us
    unnamed x10, local copies, waits for them, and re-layouts  2.11 us
  transfers between devices with their start and end apart: 1, of which 1 were waited for; matrix products, arithmetic and copies ran while one was open for 0% of the time, Pallas kernels for 15%

profile of v4, /device:TPU:1, one launch (start us, length us, event | category | flops | bytes accessed | tf_op | source)
XLA Modules:
  0.0 47.2 jit_solution(14306551356686142222)
XLA Ops:
  0.6 8.4 %field.1 = f32[640,4,128]{2,1,0:T(4,128)} custom-call(s32[640]{0:T(1024)} %waves_h.1, s32[640]{0:T(1024)} %order_h.1, f32[3]{0:T(128)} %decay_h.1, f32[3,640]{1,0:T(4,128)} %amp_h.1, f32[5,3,50,2,640]{4,3,2,1,0:T(2,128)} %bitcast.4, bf16[5,3,50,2,640]{4,3,2,1,0:T(2,128)(2,1)} %bitcast.6, f32[5,640,640]{2,1,0:T(8,128)} %leg_h.1), custom_call_target="tpu_custom_call" | custom-call | flops 1000000000 | bytes 14000000 | tf_op jit(solution)/shard_map/field/pallas_call | solution.py:329
  9.0 0.0 copy-start.3
  9.0 0.0 copy-start.1
  9.1 0.0 copy-start.2
  9.1 0.0 copy-start.4
  9.1 11.5 %all-to-all-start = ((f32[640,4,128]{2,1,0:T(4,128)}), f32[640,4,128]{2,1,0:T(4,128)S(1)}, u32[]{:S(2)}, u32[]{:S(2)}) async-start(f32[640,4,128]{2,1,0:T(4,128)} %field.1), calls=%async_computation | async-start | bytes 2621440 | tf_op jit(solution)/shard_map/exchange/all_to_all | solution.py:409
  20.6 0.0 copy-done.3
  20.6 0.2 reshape.11.wave_ref
  20.8 0.0 copy-done.1
  20.8 0.0 copy-done.2
  20.8 0.0 copy-done.4
  20.8 0.0 copy-start
  20.8 2.1 %copy-done = f32[5,2,3,50,640]{4,1,3,2,0:T(2,128)S(1)} copy-done((f32[5,2,3,50,640]{4,1,3,2,0:T(2,128)S(1)}, f32[5,2,3,50,640]{4,1,3,2,0:T(2,128)}, u32[]{:S(2)}) %copy-start) | copy-done | bytes 3840024
  22.9 7.0 %evolve.1 = f32[5,3,50,2,640]{4,3,2,1,0:T(2,128)} custom-call(s32[640]{0:T(1024)S(1)} %copy-done.3, f32[3]{0:T(128)S(1)} %copy-done.4, f32[3,640]{1,0:T(4,128)S(1)} %copy-done.2, f32[5,3,50,2,640]{4,3,2,1,0:T(2,128)S(1)} %bitcast.5, bf16[5,3,50,2,640]{4,3,2,1,0:T(2,128)(2,1)S(1)} %bitcast.7), custom_call_target="tpu_custom_call" | custom-call | flops 500000000 | bytes 10000000 | tf_op jit(solution)/shard_map/evolve/pallas_call | solution.py:359
  29.9 13.0 %all-to-all-done = f32[640,4,128]{2,1,0:T(4,128)S(1)} async-done(((f32[640,4,128]{2,1,0:T(4,128)}), f32[640,4,128]{2,1,0:T(4,128)S(1)}, u32[]{:S(2)}, u32[]{:S(2)}) %all-to-all-start) | async-done | bytes 1310752 | tf_op jit(solution)/shard_map/exchange/all_to_all | solution.py:409
  42.9 4.2 %synthesis.1 = f32[5,50,1280]{2,1,0:T(8,128)} custom-call(f32[2560,128]{1,0:T(8,128)S(1)} %bitcast.8, s32[128,5]{1,0:T(8,128)S(1)} %reshape.11.wave_ref), custom_call_target="tpu_custom_call" | custom-call | tf_op jit(solution)/shard_map/synthesis/pallas_call | solution.py:378
Async XLA Ops:
  9.0 11.6 %copy-start.3 = (s32[640]{0:T(1024)S(1)}, s32[640]{0:T(1024)}, u32[]{:S(2)}) copy-start(s32[640]{0:T(1024)} %waves_h.1) | copy-start | bytes 7684
  9.0 11.7 %copy-start.1 = (bf16[5,2,3,50,640]{4,1,3,2,0:T(2,128)(2,1)S(1)}, bf16[5,2,3,50,640]{4,1,3,2,0:T(2,128)(2,1)}, u32[]{:S(2)}) copy-start(bf16[5,2,3,50,640]{4,1,3,2,0:T(2,128)(2,1)} %param.8) | copy-start | bytes 5760004
  9.1 11.7 %copy-start.2 = (f32[3,640]{1,0:T(4,128)S(1)}, f32[3,640]{1,0:T(4,128)}, u32[]{:S(2)}) copy-start(f32[3,640]{1,0:T(4,128)} %amp_h.1) | copy-start | bytes 23044
  9.1 11.7 %copy-start.4 = (f32[3]{0:T(128)S(1)}, f32[3]{0:T(128)}, u32[]{:S(2)}) copy-start(f32[3]{0:T(128)} %decay_h.1) | copy-start | bytes 40
  9.1 33.8 %all-to-all-start = ((f32[640,4,128]{2,1,0:T(4,128)}), f32[640,4,128]{2,1,0:T(4,128)S(1)}, u32[]{:S(2)}, u32[]{:S(2)}) async-start(f32[640,4,128]{2,1,0:T(4,128)} %field.1), calls=%async_computation | async-start | bytes 2621440 | tf_op jit(solution)/shard_map/exchange/all_to_all | solution.py:409
  20.8 2.1 %copy-start = (f32[5,2,3,50,640]{4,1,3,2,0:T(2,128)S(1)}, f32[5,2,3,50,640]{4,1,3,2,0:T(2,128)}, u32[]{:S(2)}) copy-start(f32[5,2,3,50,640]{4,1,3,2,0:T(2,128)} %param.7) | copy-start | bytes 11520004
